TPU v7x, 32 devices: a whole 2x2x4 slice. The times are simulated.
32 devices in a mesh: segment: 4 (over x, core), dp: 8 (over z, y).
Axes of the slice: x: 2, y: 2, z: 4, core: 2. Of those that a mesh axis runs over, the one named last changes fastest.
Arguments:
- embeds: bfloat16 [2, 8, 128, 4096], P(None, 'dp'), may hold values from -6 to 6
- base_weight: bfloat16 [4, 4096, 4096], P('segment', 'dp'), may hold values from -0.09375 to 0.09375
- norm_gain: float32 [4, 4096], P('segment'), may hold values from 0.25 to 1.75
- skill_down: bfloat16 [4, 16, 8, 4096], P('segment'), may hold values from -0.09375 to 0.09375
- skill_up: bfloat16 [4, 16, 8, 4096], P('segment'), may hold values from -2 to 2
- task_ids: int32 [2, 8], replicated, may hold values from 0 to 1835
- allocation: int32 [1836, 16], replicated, may hold values 0 or 1
- target_lengths: int32 [2, 8], replicated, may hold values from 1 to 128
- cotangent: bfloat16 [2, 8, 128, 4096], P(None, 'dp'), may hold values from -6 to 6
Outputs:
- hidden: bfloat16 [4, 2, 8, 128, 4096], P('segment', None, 'dp')
- input_grads: bfloat16 [4, 2, 8, 128, 4096], P('segment', None, 'dp')
- grad_down: float32 [4, 16, 8, 4096], P('segment', None, None, 'dp')
- grad_up: float32 [4, 16, 8, 4096], P('segment', None, None, 'dp')
All inputs are finite; a program needn't handle non-finite values.
Results may differ from a plain program's by a relative error of at most 0.019.
Values may be sent and summed in bfloat16 or wider, within the bound.
No kernel may reach another device: no remote copies, remote signals or barrier semaphores. Data moves between devices by JAX's collectives and lax.ppermute only.
A program may use at most 192 MiB of HBM per device.

v0:
```python
import jax
import jax.numpy as jnp
from jax import lax
from jax.sharding import PartitionSpec as P

EPS = 1e-06


def shifted(block, axis, distance):
    devices = range(lax.axis_size(axis))
    route = [(i - distance, i) for i in devices if i - distance in devices]
    return lax.ppermute(block, axis, route)


def prepare(x, gain, down_t):
    xf = x.astype(jnp.float32)
    inv = lax.rsqrt(jnp.mean(xf * xf, axis=-1, keepdims=True) + EPS)
    normed = (xf * inv * gain).astype(jnp.bfloat16)
    low = jnp.dot(normed, down_t.T, preferred_element_type=jnp.float32).astype(jnp.bfloat16)
    return (normed, low, inv)


def forward_full(x, weight, gain, down_t, up_t):
    normed, low, inv = prepare(x, gain, down_t)
    total = x.astype(jnp.float32) + jnp.dot(normed, weight, preferred_element_type=jnp.float32)
    total = total + jnp.dot(low, up_t, preferred_element_type=jnp.float32)
    return (total.astype(jnp.bfloat16), normed, low, inv)


def backward_core(x, normed, low, inv, grad_out, weight, gain, down_t, up_t):
    g_low = jnp.dot(grad_out, up_t.T, preferred_element_type=jnp.float32).astype(jnp.bfloat16)
    dnorm = jnp.dot(grad_out, weight.T, preferred_element_type=jnp.float32)
    dnorm = dnorm + jnp.dot(g_low, down_t, preferred_element_type=jnp.float32)
    seq_down = jnp.dot(g_low.T, normed, preferred_element_type=jnp.float32)
    seq_up = jnp.dot(low.T, grad_out, preferred_element_type=jnp.float32)
    xf = x.astype(jnp.float32)
    scaled = gain * dnorm
    grad_in = (
        grad_out.astype(jnp.float32)
        + inv * scaled
        - xf * inv * inv * inv * jnp.mean(xf * scaled, axis=-1, keepdims=True)
    )
    return (grad_in.astype(jnp.bfloat16), seq_down, seq_up)


def pick(table, index):
    return lax.dynamic_index_in_dim(table, index, 0, keepdims=False)


def place(table, value, index, active):
    return jnp.where(active, lax.dynamic_update_index_in_dim(table, value, index, 0), table)


def shards(
    embeds,
    base_weight,
    norm_gain,
    skill_down,
    skill_up,
    task_ids,
    allocation,
    target_lengths,
    cotangent,
):
    segments = lax.axis_size("segment")
    segment = lax.axis_index("segment")
    member = lax.axis_index("dp")
    weight = lax.all_gather(base_weight[0], "dp", axis=0, tiled=True)
    gain = norm_gain[0]
    micro = embeds.shape[0]
    rows = embeds.shape[2]
    width = embeds.shape[3]
    splits = 1
    blocks = micro * splits
    block_rows = rows // splits
    tasks = lax.dynamic_index_in_dim(task_ids, member, 1, keepdims=False)
    lengths = lax.dynamic_index_in_dim(target_lengths, member, 1, keepdims=False)
    onehot = (tasks[:, None] == jnp.arange(allocation.shape[0], dtype=jnp.int32)[None, :]).astype(
        jnp.float32
    )
    alloc = allocation.astype(jnp.float32)
    counts = jnp.maximum(jnp.sum(alloc, axis=1, keepdims=True), 1.0)
    mix = jnp.einsum("mt,ts->ms", onehot, alloc / counts, precision=lax.Precision.HIGHEST)
    down_seq = jnp.einsum(
        "ms,srd->mrd", mix, skill_down[0].astype(jnp.float32), precision=lax.Precision.HIGHEST
    ).astype(jnp.bfloat16)
    up_seq = jnp.einsum(
        "ms,srd->mrd", mix, skill_up[0].astype(jnp.float32), precision=lax.Precision.HIGHEST
    ).astype(jnp.bfloat16)
    down_all = jnp.repeat(down_seq, splits, axis=0)
    up_all = jnp.repeat(up_seq, splits, axis=0)
    mix_all = jnp.repeat(mix, splits, axis=0)
    firsts = embeds[:, 0]
    live = jnp.arange(rows, dtype=jnp.int32)[None, :] < lengths[:, None]
    seeds = cotangent[:, 0] * live[..., None].astype(jnp.bfloat16)
    ticks = segments + blocks - 1
    rank = down_all.shape[1]
    blank = jnp.zeros((block_rows, width), jnp.bfloat16)
    stack_blank = jnp.zeros((blocks, block_rows, width), jnp.bfloat16)
    low_blank = jnp.zeros((blocks, block_rows, rank), jnp.bfloat16)
    inv_blank = jnp.zeros((blocks, block_rows, 1), jnp.float32)

    def forward_tick(tick, carry):
        incoming, saved, outs, kept_norm, kept_low, kept_inv = carry
        slot = tick - segment
        active = (slot >= 0) & (slot < blocks)
        index = jnp.clip(slot, 0, blocks - 1)
        x = jnp.where(segment == 0, pick(firsts, index), incoming)
        result, normed, low, inv = lax.cond(
            active,
            lambda: forward_full(x, weight, gain, pick(down_all, index), pick(up_all, index)),
            lambda: (
                blank,
                blank,
                jnp.zeros((block_rows, rank), jnp.bfloat16),
                jnp.zeros((block_rows, 1), jnp.float32),
            ),
        )
        saved = place(saved, x, index, active)
        outs = place(outs, result, index, active)
        return (result, (saved, outs, kept_norm, kept_low, kept_inv))

    def forward_step(tick, carry):
        result, rest = forward_tick(tick, carry)
        moved = shifted(result, "segment", 1)
        return (moved,) + rest

    carry = (blank, stack_blank, stack_blank, stack_blank, low_blank, inv_blank)
    carry = lax.fori_loop(0, ticks - 1, forward_step, carry)
    _, (saved, outs, kept_norm, kept_low, kept_inv) = forward_tick(ticks - 1, carry)
    skills = skill_down.shape[1]
    acc_blank = jnp.zeros((skills, rank, width), jnp.float32)

    def backward_tick(tick, carry):
        incoming, grads_in, acc_down, acc_up = carry
        slot = tick - (segments - 1 - segment)
        active = (slot >= 0) & (slot < blocks)
        index = jnp.clip(slot, 0, blocks - 1)
        grad_out = jnp.where(segment == segments - 1, pick(seeds, index), incoming)
        x = pick(saved, index)
        down_t = pick(down_all, index)
        up_t = pick(up_all, index)

        def run():
            normed, low, inv = prepare(x, gain, down_t)
            return backward_core(x, normed, low, inv, grad_out, weight, gain, down_t, up_t)

        grad_in, seq_down, seq_up = lax.cond(
            active,
            run,
            lambda: (
                blank,
                jnp.zeros((rank, width), jnp.float32),
                jnp.zeros((rank, width), jnp.float32),
            ),
        )
        weights = pick(mix_all, index)[:, None, None]
        acc_down = acc_down + weights * seq_down[None]
        acc_up = acc_up + weights * seq_up[None]
        grads_in = place(grads_in, grad_in, index, active)
        return (grad_in, (grads_in, acc_down, acc_up))

    def backward_step(tick, carry):
        grad_in, rest = backward_tick(tick, carry)
        moved = shifted(grad_in, "segment", -1)
        return (moved,) + rest

    carry = (blank, stack_blank, acc_blank, acc_blank)
    carry = lax.fori_loop(0, ticks - 1, backward_step, carry)
    _, (grads_in, acc_down, acc_up) = backward_tick(ticks - 1, carry)
    grad_down, grad_up = (
        lax.psum_scatter(
            acc_down.astype(jnp.bfloat16), "dp", scatter_dimension=2, tiled=True
        ).astype(jnp.float32),
        lax.psum_scatter(acc_up.astype(jnp.bfloat16), "dp", scatter_dimension=2, tiled=True).astype(
            jnp.float32
        ),
    )
    return (outs[None, :, None], grads_in[None, :, None], grad_down[None], grad_up[None])


def solution(mesh):
    in_specs = (
        P(None, "dp", None, None),
        P("segment", "dp", None),
        P("segment", None),
        P("segment", None, None, None),
        P("segment", None, None, None),
        P(),
        P(),
        P(),
        P(None, "dp", None, None),
    )
    out_specs = (
        P("segment", None, "dp", None, None),
        P("segment", None, "dp", None, None),
        P("segment", None, None, "dp"),
        P("segment", None, None, "dp"),
    )
    return jax.shard_map(shards, mesh=mesh, in_specs=in_specs, out_specs=out_specs, check_vma=False)
```

profile of v0, /device:TPU:1, one launch (start us, length us, event | category | flops | bytes accessed | tf_op | source)
XLA Modules:
  0.0 1099.3 jit_solution(8175166725081357591)
XLA Ops:
  8.5 1.6 convolution_convert_fusion.5
  10.2 2.8 convolution_convert_fusion.4
  16.1 633.0 %all-gather.3.cloned.1.call-done = bf16[1,4096,4096]{2,1,0:T(8,128)(2,1)} async-done(((bf16[1,512,4096]{2,1,0:T(8,128)(2,1)}), bf16[1,4096,4096]{2,1,0:T(8,128)(2,1)}) %all-gather.3.cloned.1.call-update) | async-done | bytes 33554448 | tf_op jit(solution)/shard_map/all_gather | solution.py:68
  652.1 139.9 %while.40 = (s32[]{:T(128)}, bf16[128,4096]{1,0:T(8,128)(2,1)}, bf16[2,128,4096]{2,1,0:T(8,128)(2,1)S(1)}, bf16[2,128,4096]{2,1,0:T(8,128)(2,1)}, s32[]{:T(128)}...) while((s32[]{:T(128)}, bf16[128,4096]{1,0:T(8,128)(2,1)}, ...), condition=%wide.region_5.6_spmd, body=%wide.region_1.5_spmd.sunk | while | flops 4321182720 | bytes 77762976 | solution.py:129
  652.1 2.1 fusion.171
  656.7 3.9 collective-permute-start
  660.7 2.5 select_dynamic-update-slice_fusion.4
  663.2 15.4 %collective-permute-done = bf16[128,4096]{1,0:T(8,128)(2,1)} collective-permute-done((bf16[128,4096]{1,0:T(8,128)(2,1)S(1)}, bf16[128,4096]{1,0:T(8,128)(2,1)}, u32[]{:S(2)}, u32[]{:S(2)}) %collective-permute-start) | collective-permute-done | bytes 1048608 | tf_op jit(solution)/shard_map/while/body/eval_jaxpr/ppermute | solution.py:12
  678.6 2.1 fusion.171
  682.1 18.8 %conditional.9 = (bf16[128,4096]{1,0:T(8,128)(2,1)S(1)}, bf16[1,128,4096]{2,1,0:T(8,128)(2,1)}) conditional(s32[]{:T(128)} %convert_element_type.342, () %tuple.144, (bf16[128,4096]{1,0:T(8,128)(2,1)S(1)}, f32[1,4096]{1,0:T(1,128)S(1)}, bf16[4096,4096]{1,0:T(8,128)(2,1)}, s32[]{:T(128)}, bf16[2,8,4096]{2,1,0:T(8,128)(2,1)S(1)}, ...), branch_computations={%region_2.2_spmd, %region_3.4_spmd} | conditional | flops 4319609856 | bytes 48401996 | solution.py:109
  682.4 13.0 %convolution_add_fusion.1 = f32[128,4096]{1,0:T(8,128)S(1)} fusion(bf16[4096,4096]{1,0:T(8,128)(2,1)} %get-tuple-element.684, bf16[128,4096]{1,0:T(8,128)(2,1)S(1)} %get-tuple-element.682, f32[4096]{0:T(1024)S(1)} %bitcast.180, f32[128]{0:T(128)S(1)} %add_rsqrt_fusion), kind=kOutput, calls=%fused_computation.1 | convolution fusion | flops 4298113024 | bytes 36717056 | tf_op jit(solution)/shard_map/while/body/eval_jaxpr/cond/branch_1_fun/dot_general | solution.py:25
  695.3 3.2 fusion
  698.5 2.4 copy.31
  700.9 2.0 collective-permute-start
  703.0 2.8 select_dynamic-update-slice_fusion.4
  705.8 8.9 collective-permute-done
  714.7 2.1 fusion.171
  718.1 18.8 %conditional.9 = (bf16[128,4096]{1,0:T(8,128)(2,1)S(1)}, bf16[1,128,4096]{2,1,0:T(8,128)(2,1)}) conditional(s32[]{:T(128)} %convert_element_type.342, () %tuple.144, (bf16[128,4096]{1,0:T(8,128)(2,1)S(1)}, f32[1,4096]{1,0:T(1,128)S(1)}, bf16[4096,4096]{1,0:T(8,128)(2,1)}, s32[]{:T(128)}, bf16[2,8,4096]{2,1,0:T(8,128)(2,1)S(1)}, ...), branch_computations={%region_2.2_spmd, %region_3.4_spmd} | conditional | flops 4319609856 | bytes 48401996 | solution.py:109
  718.4 13.0 %convolution_add_fusion.1 = f32[128,4096]{1,0:T(8,128)S(1)} fusion(bf16[4096,4096]{1,0:T(8,128)(2,1)} %get-tuple-element.684, bf16[128,4096]{1,0:T(8,128)(2,1)S(1)} %get-tuple-element.682, f32[4096]{0:T(1024)S(1)} %bitcast.180, f32[128]{0:T(128)S(1)} %add_rsqrt_fusion), kind=kOutput, calls=%fused_computation.1 | convolution fusion | flops 4298113024 | bytes 36717056 | tf_op jit(solution)/shard_map/while/body/eval_jaxpr/cond/branch_1_fun/dot_general | solution.py:25
  731.4 3.2 fusion
  734.6 2.4 copy.31
  737.0 4.6 collective-permute-start
  741.6 2.8 select_dynamic-update-slice_fusion.4
  744.4 9.0 collective-permute-done
  753.3 2.1 fusion.171
  758.0 22.3 %collective-permute-start = (bf16[128,4096]{1,0:T(8,128)(2,1)S(1)}, bf16[128,4096]{1,0:T(8,128)(2,1)}, u32[]{:S(2)}, u32[]{:S(2)}) collective-permute-start(bf16[128,4096]{1,0:T(8,128)(2,1)S(1)} %get-tuple-element.1077), channel_id=1, source_target_pairs={{0,8},{8,16},{16,24},{1,9},{9,17},{17,25},{2,10},{10,18},{18,26},{... | collective-permute-start | bytes 3145736 | tf_op jit(solution)/shard_map/while/body/eval_jaxpr/ppermute | solution.py:12
  780.3 2.4 select_dynamic-update-slice_fusion.4
  782.7 9.3 collective-permute-done
  792.0 3.1 fusion.140
  797.8 149.5 %while.41 = (s32[]{:T(128)}, bf16[128,4096]{1,0:T(8,128)(2,1)}, bf16[2,128,4096]{2,1,0:T(8,128)(2,1)}, f32[16,8,4096]{2,1,0:T(8,128)}, f32[16,8,4096]{2,1,0:T(8,...) while((s32[]{:T(128)}, bf16[128,4096]{1,0:T(8,128)(2,1)}, ...), condition=%wide.region_14.15_spmd.clone, body=%wide.region_9.14_spmd.clone.sunk | while | flops 4354214400 | bytes 94118616 | solution.py:169
  797.8 2.2 conditional.10
  800.0 1.9 collective-permute-start.1
  802.8 2.4 select_dynamic-update-slice_fusion.5
  805.3 2.8 select_add_fusion.3
  808.0 9.2 collective-permute-done.1
  818.3 2.2 conditional.10
  820.5 1.9 collective-permute-start.1
  823.3 2.4 select_dynamic-update-slice_fusion.5
  825.7 4.4 select_add_fusion.3
  830.1 29.6 %collective-permute-done.1 = bf16[128,4096]{1,0:T(8,128)(2,1)S(1)} collective-permute-done((bf16[128,4096]{1,0:T(8,128)(2,1)}, bf16[128,4096]{1,0:T(8,128)(2,1)S(1)}, u32[]{:S(2)}, u32[]{:S(2)}) %collective-permute-start.1) | collective-permute-done | bytes 1048608 | tf_op jit(solution)/shard_map/while/body/eval_jaxpr/ppermute | solution.py:12
  860.7 25.9 %conditional.10 = (bf16[128,4096]{1,0:T(8,128)(2,1)}, f32[8,4096]{1,0:T(8,128)S(1)}, f32[8,4096]{1,0:T(8,128)S(1)}, bf16[1,128,4096]{2,1,0:T(8,128)(2,1)}) conditional(s32[]{:T(128)} %convert_element_type.343, () %tuple.148, (pred[]{:T(512)}, bf16[2,128,4096]{2,1,0:T(8,128)(2,1)}, s32[]{:T(128)}, bf16[128,4096]{1,0:T(8,128)(2,1)}, ...), branch_computations={%region_10.10_spmd, %region_11.13_spmd} | conditional | flops 4350544384 | bytes 57155172 | solution.py:148
  860.7 1.7 bitcast_select_fusion.2
  863.6 16.0 %fusion.153 = f32[128,4096]{1,0:T(8,128)S(1)} fusion(bf16[128,4096]{1,0:T(8,128)(2,1)S(1)} %bitcast_select_fusion.2, bf16[4096,4096]{1,0:T(8,128)(2,1)} %get-tuple-element.714), kind=kOutput, calls=%fused_computation.166 | convolution fusion | flops 4294967296 | bytes 36700160 | tf_op jit(solution)/shard_map/while/body/eval_jaxpr/cond/branch_1_fun/dot_general | solution.py:32
  880.4 1.8 fusion.61
  882.2 2.3 copy.40
  886.7 1.9 collective-permute-start.1
  889.4 2.8 select_dynamic-update-slice_fusion.5
  892.2 4.4 select_add_fusion.3
  896.6 6.4 collective-permute-done.1
  904.0 25.9 %conditional.10 = (bf16[128,4096]{1,0:T(8,128)(2,1)}, f32[8,4096]{1,0:T(8,128)S(1)}, f32[8,4096]{1,0:T(8,128)S(1)}, bf16[1,128,4096]{2,1,0:T(8,128)(2,1)}) conditional(s32[]{:T(128)} %convert_element_type.343, () %tuple.148, (pred[]{:T(512)}, bf16[2,128,4096]{2,1,0:T(8,128)(2,1)}, s32[]{:T(128)}, bf16[128,4096]{1,0:T(8,128)(2,1)}, ...), branch_computations={%region_10.10_spmd, %region_11.13_spmd} | conditional | flops 4350544384 | bytes 57155172 | solution.py:148
  904.0 1.7 bitcast_select_fusion.2
  906.9 16.0 %fusion.153 = f32[128,4096]{1,0:T(8,128)S(1)} fusion(bf16[128,4096]{1,0:T(8,128)(2,1)S(1)} %bitcast_select_fusion.2, bf16[4096,4096]{1,0:T(8,128)(2,1)} %get-tuple-element.714), kind=kOutput, calls=%fused_computation.166 | convolution fusion | flops 4294967296 | bytes 36700160 | tf_op jit(solution)/shard_map/while/body/eval_jaxpr/cond/branch_1_fun/dot_general | solution.py:32
  923.7 1.8 fusion.61
  925.5 2.3 copy.40
  930.0 1.9 collective-permute-start.1
  932.7 2.8 select_dynamic-update-slice_fusion.5
  935.5 4.4 select_add_fusion.3
  939.9 6.4 collective-permute-done.1
  948.7 4.2 add_convert_fusion
  959.5 3.4 bitcast_dynamic-update-slice_fusion
  962.9 61.0 %reduce-scatter.5.cloned.1.call-done = bf16[16,8,512]{2,1,0:T(8,128)(2,1)} async-done(((bf16[16,8,4096]{2,1,0:T(8,128)(2,1)}), bf16[16,8,512]{2,1,0:T(8,128)(2,1)}) %reduce-scatter.5.cloned.1.call-update) | async-done | bytes 131088 | tf_op jit(solution)/shard_map/reduce_scatter | solution.py:175
  1024.0 1.6 bitcast_convert_fusion
  1025.6 65.5 %reduce-scatter.3.cloned.1.call-done = bf16[16,8,512]{2,1,0:T(8,128)(2,1)} async-done(((bf16[16,8,4096]{2,1,0:T(8,128)(2,1)}), bf16[16,8,512]{2,1,0:T(8,128)(2,1)}) %reduce-scatter.3.cloned.1.call-update) | async-done | bytes 131088 | tf_op jit(solution)/shard_map/reduce_scatter | solution.py:172
  1091.1 1.6 bitcast_convert_fusion.1
  (145 shorter events, 51.0 us)
Async XLA Ops:
  7.2 1.3 copy-start
  7.2 0.9 copy-start.24
  7.2 1.1 copy-start.20
  7.2 641.9 %all-gather.3.cloned.1.call-start = ((), (), s32[]{:S(2)}) async-start(), calls=%async_computation.4 | async-start | bytes 37748736 | tf_op jit(solution)/shard_map/all_gather | solution.py:68
  7.9 5.8 copy-start.25
  7.9 6.6 copy-start.12
  8.0 1016.0 %reduce-scatter.5.cloned.1.call-start = ((), (), s32[]{:S(2)}) async-start(), calls=%async_computation.3 | async-start | bytes 1179648 | tf_op jit(solution)/shard_map/reduce_scatter | solution.py:175
  8.5 7.6 copy-start.23
  10.1 6.0 copy-start.13
  13.0 3.1 copy-start.16
  649.4 2.7 copy-start.11
  654.2 1.3 copy-start.2
  656.7 21.9 %copy-start.3 = (bf16[2,128,4096]{2,1,0:T(8,128)(2,1)S(1)}, bf16[2,128,4096]{2,1,0:T(8,128)(2,1)}, u32[]{:S(2)}) copy-start(bf16[2,128,4096]{2,1,0:T(8,128)(2,1)} %copy-done.2) | copy-start | bytes 6291460 | tf_op jit(solution)/shard_map/while
  656.7 21.9 %collective-permute-start = (bf16[128,4096]{1,0:T(8,128)(2,1)S(1)}, bf16[128,4096]{1,0:T(8,128)(2,1)}, u32[]{:S(2)}, u32[]{:S(2)}) collective-permute-start(bf16[128,4096]{1,0:T(8,128)(2,1)S(1)} %get-tuple-element.1077), channel_id=1, source_target_pairs={{0,8},{8,16},{16,24},{1,9},{9,17},{17,25},{2,10},{10,18},{18,26},{... | collective-permute-start | bytes 3145736 | tf_op jit(solution)/shard_map/while/body/eval_jaxpr/ppermute | solution.py:12
  680.7 1.3 copy-start.2
  698.5 2.4 copy-start.4
  700.9 13.8 %copy-start.3 = (bf16[2,128,4096]{2,1,0:T(8,128)(2,1)S(1)}, bf16[2,128,4096]{2,1,0:T(8,128)(2,1)}, u32[]{:S(2)}) copy-start(bf16[2,128,4096]{2,1,0:T(8,128)(2,1)} %copy-done.2) | copy-start | bytes 6291460 | tf_op jit(solution)/shard_map/while
  700.9 13.8 %collective-permute-start = (bf16[128,4096]{1,0:T(8,128)(2,1)S(1)}, bf16[128,4096]{1,0:T(8,128)(2,1)}, u32[]{:S(2)}, u32[]{:S(2)}) collective-permute-start(bf16[128,4096]{1,0:T(8,128)(2,1)S(1)} %get-tuple-element.1077), channel_id=1, source_target_pairs={{0,8},{8,16},{16,24},{1,9},{9,17},{17,25},{2,10},{10,18},{18,26},{... | collective-permute-start | bytes 3145736 | tf_op jit(solution)/shard_map/while/body/eval_jaxpr/ppermute | solution.py:12
  716.8 1.3 copy-start.2
  734.6 2.4 copy-start.4
  737.0 16.4 %copy-start.3 = (bf16[2,128,4096]{2,1,0:T(8,128)(2,1)S(1)}, bf16[2,128,4096]{2,1,0:T(8,128)(2,1)}, u32[]{:S(2)}) copy-start(bf16[2,128,4096]{2,1,0:T(8,128)(2,1)} %copy-done.2) | copy-start | bytes 6291460 | tf_op jit(solution)/shard_map/while
  737.0 16.3 %collective-permute-start = (bf16[128,4096]{1,0:T(8,128)(2,1)S(1)}, bf16[128,4096]{1,0:T(8,128)(2,1)}, u32[]{:S(2)}, u32[]{:S(2)}) collective-permute-start(bf16[128,4096]{1,0:T(8,128)(2,1)S(1)} %get-tuple-element.1077), channel_id=1, source_target_pairs={{0,8},{8,16},{16,24},{1,9},{9,17},{17,25},{2,10},{10,18},{18,26},{... | collective-permute-start | bytes 3145736 | tf_op jit(solution)/shard_map/while/body/eval_jaxpr/ppermute | solution.py:12
  755.5 1.3 copy-start.2
  758.0 34.0 %copy-start.3 = (bf16[2,128,4096]{2,1,0:T(8,128)(2,1)S(1)}, bf16[2,128,4096]{2,1,0:T(8,128)(2,1)}, u32[]{:S(2)}) copy-start(bf16[2,128,4096]{2,1,0:T(8,128)(2,1)} %copy-done.2) | copy-start | bytes 6291460 | tf_op jit(solution)/shard_map/while
  758.0 34.0 %collective-permute-start = (bf16[128,4096]{1,0:T(8,128)(2,1)S(1)}, bf16[128,4096]{1,0:T(8,128)(2,1)}, u32[]{:S(2)}, u32[]{:S(2)}) collective-permute-start(bf16[128,4096]{1,0:T(8,128)(2,1)S(1)} %get-tuple-element.1077), channel_id=1, source_target_pairs={{0,8},{8,16},{16,24},{1,9},{9,17},{17,25},{2,10},{10,18},{18,26},{... | collective-permute-start | bytes 3145736 | tf_op jit(solution)/shard_map/while/body/eval_jaxpr/ppermute | solution.py:12
  800.0 17.2 %collective-permute-start.1 = (bf16[128,4096]{1,0:T(8,128)(2,1)}, bf16[128,4096]{1,0:T(8,128)(2,1)S(1)}, u32[]{:S(2)}, u32[]{:S(2)}) collective-permute-start(bf16[128,4096]{1,0:T(8,128)(2,1)} %get-tuple-element.1094), channel_id=1, source_target_pairs={{8,0},{16,8},{24,16},{9,1},{17,9},{25,17},{10,2},{18,10},{26,18},{... | collective-permute-start | bytes 3145736 | tf_op jit(solution)/shard_map/while/body/eval_jaxpr/ppermute | solution.py:12
  802.0 3.3 copy-start.5
  808.0 9.2 copy-start.6
  817.2 1.1 copy-start.9
  820.5 39.2 %collective-permute-start.1 = (bf16[128,4096]{1,0:T(8,128)(2,1)}, bf16[128,4096]{1,0:T(8,128)(2,1)S(1)}, u32[]{:S(2)}, u32[]{:S(2)}) collective-permute-start(bf16[128,4096]{1,0:T(8,128)(2,1)} %get-tuple-element.1094), channel_id=1, source_target_pairs={{8,0},{16,8},{24,16},{9,1},{17,9},{25,17},{10,2},{18,10},{26,18},{... | collective-permute-start | bytes 3145736 | tf_op jit(solution)/shard_map/while/body/eval_jaxpr/ppermute | solution.py:12
  822.4 3.3 copy-start.5
  830.1 29.6 %copy-start.6 = (f32[16,8,4096]{2,1,0:T(8,128)}, f32[16,8,4096]{2,1,0:T(8,128)S(1)}, u32[]{:S(2)}) copy-start(f32[16,8,4096]{2,1,0:T(8,128)S(1)} %get-tuple-element.1191) | copy-start | bytes 6291460 | tf_op jit(solution)/shard_map/while
  859.7 1.1 copy-start.9
  863.6 16.0 %copy-start.19 = (bf16[128,8]{0,1:T(8,128)(2,1)}, bf16[128,8]{0,1:T(8,128)(2,1)S(1)}, u32[]{:S(2)}) copy-start(bf16[128,8]{0,1:T(8,128)(2,1)S(1)} %convolution_convert_fusion.1) | copy-start | bytes 6148 | tf_op jit(solution)/shard_map/while/body/eval_jaxpr/cond
  880.4 4.1 copy-start.21
  886.7 16.3 %collective-permute-start.1 = (bf16[128,4096]{1,0:T(8,128)(2,1)}, bf16[128,4096]{1,0:T(8,128)(2,1)S(1)}, u32[]{:S(2)}, u32[]{:S(2)}) collective-permute-start(bf16[128,4096]{1,0:T(8,128)(2,1)} %get-tuple-element.1094), channel_id=1, source_target_pairs={{8,0},{16,8},{24,16},{9,1},{17,9},{25,17},{10,2},{18,10},{26,18},{... | collective-permute-start | bytes 3145736 | tf_op jit(solution)/shard_map/while/body/eval_jaxpr/ppermute | solution.py:12
  888.6 3.6 copy-start.5
  896.6 6.4 copy-start.6
  903.0 1.1 copy-start.9
  906.9 16.0 %copy-start.19 = (bf16[128,8]{0,1:T(8,128)(2,1)}, bf16[128,8]{0,1:T(8,128)(2,1)S(1)}, u32[]{:S(2)}) copy-start(bf16[128,8]{0,1:T(8,128)(2,1)S(1)} %convolution_convert_fusion.1) | copy-start | bytes 6148 | tf_op jit(solution)/shard_map/while/body/eval_jaxpr/cond
  923.7 4.1 copy-start.21
  930.0 16.3 %collective-permute-start.1 = (bf16[128,4096]{1,0:T(8,128)(2,1)}, bf16[128,4096]{1,0:T(8,128)(2,1)S(1)}, u32[]{:S(2)}, u32[]{:S(2)}) collective-permute-start(bf16[128,4096]{1,0:T(8,128)(2,1)} %get-tuple-element.1094), channel_id=1, source_target_pairs={{8,0},{16,8},{24,16},{9,1},{17,9},{25,17},{10,2},{18,10},{26,18},{... | collective-permute-start | bytes 3145736 | tf_op jit(solution)/shard_map/while/body/eval_jaxpr/ppermute | solution.py:12
  931.9 3.6 copy-start.5
  939.9 6.4 copy-start.6
  946.3 1.1 copy-start.9
  952.9 1.6 copy-start.7
  952.9 138.2 %reduce-scatter.3.cloned.1.call-start = ((), (), s32[]{:S(2)}) async-start(), calls=%async_computation.2 | async-start | bytes 1179648 | tf_op jit(solution)/shard_map/reduce_scatter | solution.py:172
  954.5 2.3 copy-start.8
  954.5 2.6 copy-start.10
  954.5 2.6 copy-start.14
  954.5 2.6 copy-start.17
  959.5 133.2 %copy-start.1 = (bf16[1,16,8,4096]{3,2,1,0:T(8,128)(2,1)S(1)}, bf16[1,16,8,4096]{3,2,1,0:T(8,128)(2,1)}, u32[]{:S(2)}) copy-start(bf16[1,16,8,4096]{3,2,1,0:T(8,128)(2,1)} %param.24) | copy-start | bytes 3145732
Sparse Core Ops, SparseCore 0:
  9.5 639.5 all-gather.2
  953.0 70.8 reduce-scatter.4
  1027.4 63.6 reduce-scatter.2
where the time goes:
time: 1100 us
  waiting for transfers between devices  855 us (78%)
  matrix products  77.1 us (7%)
  other arithmetic  68.3 us (6%)
  local copies, waits for them, and re-layouts  43.5 us (4%)
  starting transfers between devices  40.6 us (4%)
  between operations  14 us (1%)
    all_gather x1, waiting for transfers between devices, shards(): weight = lax.all_gather(base_weight[0], 'dp', axis=0, tiled=True)  633 us
    ppermute x8, waiting for transfers between devices, shifted(): return lax.ppermute(block, axis, route)  94.2 us
    reduce_scatter x1, waiting for transfers between devices, shards(): lax.psum_scatter(acc_down.astype(jnp.bfloat16), 'dp', scatter_dimension=2...  65.5 us
    reduce_scatter x1, waiting for transfers between devices, shards(): lax.psum_scatter(acc_up.astype(jnp.bfloat16), 'dp', scatter_dimension=2,...  61 us
    ppermute x8, starting transfers between devices, shifted(): return lax.ppermute(block, axis, route)  40.5 us
    select_n x14, other arithmetic, place(): jnp.where(active, lax.dynamic_update_index_in_dim(table, value, index, 0)...  35.9 us
    dot_general x2, matrix products, backward_core(): dnorm = jnp.dot(grad_out, weight.T, preferred_element_type=jnp.float32)  32 us
    dot_general x2, matrix products, forward_full(): jnp.dot(normed, weight, preferred_element_type=jnp.float32)  25.9 us
  transfers between devices with their start and end apart: 11, of which 11 were waited for; matrix products, arithmetic and copies ran while one was open for 5% of the time, Pallas kernels for 0%

commit v1 on v0

v1 whole, which is shorter than its diff:
```python
import jax
import jax.numpy as jnp
from jax import lax
from jax.sharding import PartitionSpec as P

EPS = 1e-06


def snake(count):
    inner = max(d for d in range(1, count + 1) if count % d == 0 and d * d <= count)
    outer = count // inner
    if inner == 1 or outer == 1:
        return list(range(count))
    if inner % 2:
        return [z * inner + (y if z % 2 == 0 else inner - 1 - y) for z in range(outer) for y in range(inner)]
    back = []
    for y in range(inner):
        column = [z * inner + y for z in range(1, outer)]
        back += column if y % 2 == 0 else column[::-1]
    return [y for y in range(1)] + back + [y for y in range(inner - 1, 0, -1)]


def prepare(x, gain, down):
    xf = x.astype(jnp.float32)
    inv = lax.rsqrt(jnp.mean(xf * xf, axis=-1, keepdims=True) + EPS)
    normed = (xf * inv * gain).astype(jnp.bfloat16)
    low = jnp.einsum("mtd,mrd->mtr", normed, down, preferred_element_type=jnp.float32).astype(jnp.bfloat16)
    return (normed, low, inv)


def wide(rows, weight):
    flat = rows.reshape(-1, rows.shape[-1])
    return jnp.dot(flat, weight, preferred_element_type=jnp.float32).reshape(rows.shape[:-1] + (weight.shape[1],))


def forward(x, weight, gain, down, up):
    normed, low, inv = prepare(x, gain, down)
    total = x.astype(jnp.float32) + wide(normed, weight)
    total = total + jnp.einsum("mtr,mrd->mtd", low, up, preferred_element_type=jnp.float32)
    return total.astype(jnp.bfloat16)


def backward(x, inv, grad, weight, gain, down, up):
    g_low = jnp.einsum("mtd,mrd->mtr", grad, up, preferred_element_type=jnp.float32).astype(jnp.bfloat16)
    dnorm = wide(grad, weight.T)
    dnorm = dnorm + jnp.einsum("mtr,mrd->mtd", g_low, down, preferred_element_type=jnp.float32)
    xf = x.astype(jnp.float32)
    scaled = gain * dnorm
    grad_in = (
        grad.astype(jnp.float32)
        + inv * scaled
        - xf * inv * inv * inv * jnp.mean(xf * scaled, axis=-1, keepdims=True)
    )
    return grad_in.astype(jnp.bfloat16)


def sequence_grads(normed, low, grad, up):
    g_low = jnp.einsum("mtd,mrd->mtr", grad, up, preferred_element_type=jnp.float32).astype(jnp.bfloat16)
    seq_down = jnp.einsum("mtr,mtd->mrd", g_low, normed, preferred_element_type=jnp.float32)
    seq_up = jnp.einsum("mtr,mtd->mrd", low, grad, preferred_element_type=jnp.float32)
    return seq_down, seq_up


def shards(
    embeds,
    base_weight,
    norm_gain,
    skill_down,
    skill_up,
    task_ids,
    allocation,
    target_lengths,
    cotangent,
):
    segments = lax.axis_size("segment")
    members = lax.axis_size("dp")
    segment = lax.axis_index("segment")
    member = lax.axis_index("dp")
    order = snake(members)
    gathered = lax.all_gather(base_weight[0], "dp", axis=0, axis_index_groups=[order])
    place_of = [order.index(j) for j in range(members)]
    weight = jnp.concatenate([gathered[p] for p in place_of], axis=0)
    gain = norm_gain[0]
    rows = embeds.shape[2]
    width = embeds.shape[3]
    onehot = (task_ids[..., None] == jnp.arange(allocation.shape[0], dtype=jnp.int32)).astype(jnp.float32)
    alloc = allocation.astype(jnp.float32)
    counts = jnp.maximum(jnp.sum(alloc, axis=1, keepdims=True), 1.0)
    mix_all = jnp.einsum("mjt,ts->mjs", onehot, alloc / counts, precision=lax.Precision.HIGHEST)
    mix = lax.dynamic_index_in_dim(mix_all, member, 1, keepdims=False)
    lengths = lax.dynamic_index_in_dim(target_lengths, member, 1, keepdims=False)
    down = jnp.einsum(
        "ms,srd->mrd", mix, skill_down[0].astype(jnp.float32), precision=lax.Precision.HIGHEST
    ).astype(jnp.bfloat16)
    up = jnp.einsum(
        "ms,srd->mrd", mix, skill_up[0].astype(jnp.float32), precision=lax.Precision.HIGHEST
    ).astype(jnp.bfloat16)
    live = jnp.arange(rows, dtype=jnp.int32)[None, :] < lengths[:, None]
    x = embeds[:, 0]
    for k in range(segments - 1):
        result = forward(x, weight, gain, down, up)
        moved = lax.ppermute(result, "segment", [(k, k + 1)])
        x = jnp.where(segment == k + 1, moved, x)
    hidden = forward(x, weight, gain, down, up)
    normed, low, inv = prepare(x, gain, down)
    grad = cotangent[:, 0] * live[..., None].astype(jnp.bfloat16)
    for k in range(segments - 1, 0, -1):
        result = backward(x, inv, grad, weight, gain, down, up)
        moved = lax.ppermute(result, "segment", [(k, k - 1)])
        grad = jnp.where(segment == k - 1, moved, grad)
    both = jnp.stack(sequence_grads(normed, low, grad, up)).astype(jnp.bfloat16)
    split = both.reshape(both.shape[:-1] + (members, width // members))
    parts = lax.all_to_all(split, "dp", split_axis=split.ndim - 2, concat_axis=0)
    grad_in = backward(x, inv, grad, weight, gain, down, up)
    mixed = jnp.einsum("mjs,jfmrd->fjsrd", mix_all, parts.astype(jnp.float32), precision=lax.Precision.HIGHEST)
    total = jnp.sum(mixed.astype(jnp.bfloat16).astype(jnp.float32), axis=1)
    return (hidden[None, :, None], grad_in[None, :, None], total[0][None], total[1][None])


def solution(mesh):
    in_specs = (
        P(None, "dp", None, None),
        P("segment", "dp", None),
        P("segment", None),
        P("segment", None, None, None),
        P("segment", None, None, None),
        P(),
        P(),
        P(),
        P(None, "dp", None, None),
    )
    out_specs = (
        P("segment", None, "dp", None, None),
        P("segment", None, "dp", None, None),
        P("segment", None, None, "dp"),
        P("segment", None, None, "dp"),
    )
    return jax.shard_map(shards, mesh=mesh, in_specs=in_specs, out_specs=out_specs, check_vma=False)
```

time: 1100 us -> 689 us (0.63)
  waiting for transfers between devices: 855 us -> 381 us
  matrix products: 77.1 us -> 189 us
  other arithmetic: 68.3 us -> 38.4 us
  starting transfers between devices: 40.6 us -> 16.6 us
    all_gather x1, waiting for transfers between devices: 633 us -> 321 us  [shards(): lax.all_gather(base_weight[0], 'dp', axis=0, axis_index_groups=[order])]
    reduce_scatter x2 -> x0, waiting for transfers between devices: 127 us -> none  [the longest x1 65.5 us: shards(): lax.psum_scatter(acc_down.astype(jnp.bfloat16), 'dp', scatter_dimension=2...]
    dot_general x15 -> x22, matrix products: 72.7 us -> 184 us  [the longest x8 144 us: wide(): jnp.dot(flat, weight, preferred_element_type=jnp.float32)]
    ppermute x8 -> x6, waiting for transfers between devices: 94.2 us -> 59.4 us  [the longest x3 32.8 us: shards(): moved = lax.ppermute(result, 'segment', [(k, k - 1)])]
    select_n x16 -> x3, other arithmetic: 39.2 us -> 6.54 us  [shards(): grad = jnp.where(segment == k - 1, moved, grad)]
    unnamed x32 -> x41, local copies, waits for them, and re-layouts: 4.84 us -> 35.6 us
    ppermute x8 -> x6, starting transfers between devices: 40.5 us -> 11.9 us  [the longest x3 6.6 us: shards(): moved = lax.ppermute(result, 'segment', [(k, k + 1)])]
    add x4 -> x0, other arithmetic: 15.9 us -> none  [backward_tick(): acc_up = acc_up + weights * seq_up[None]]
  transfers between devices with their start and end apart: 11 -> 8, of which waited for: 11 -> 4; matrix products, arithmetic and copies ran while one was open for 5% -> 11% of each run, Pallas kernels for 0% -> 0%
where the time goes in v1:
time: 689 us; the launch traced here: 680 us
  waiting for transfers between devices  381 us (55%)
  matrix products  189 us (27%)
  local copies, waits for them, and re-layouts  40.8 us (6%)
  other arithmetic  38.4 us (6%)
  starting transfers between devices  16.6 us (2%)
  between operations  14.8 us (2%)
    all_gather x1, waiting for transfers between devices, shards(): lax.all_gather(base_weight[0], 'dp', axis=0, axis_index_groups=[order])  321 us
    dot_general x8, matrix products, wide(): jnp.dot(flat, weight, preferred_element_type=jnp.float32)  144 us
    unnamed x41, local copies, waits for them, and re-layouts  35.6 us
    ppermute x3, waiting for transfers between devices, shards(): moved = lax.ppermute(result, 'segment', [(k, k - 1)])  32.8 us
    ppermute x3, waiting for transfers between devices, shards(): moved = lax.ppermute(result, 'segment', [(k, k + 1)])  26.6 us
    dot_general x4, matrix products, backward(): jnp.einsum('mtr,mrd->mtd', g_low, down, preferred_element_type=jnp.float32)  18.1 us
    dot_general x4, matrix products, forward(): jnp.einsum('mtr,mrd->mtd', low, up, preferred_element_type=jnp.float32)  17.9 us
    convert_element_type x3, other arithmetic, backward(): return grad_in.astype(jnp.bfloat16)  13.8 us
  transfers between devices with their start and end apart: 8, of which 4 were waited for; matrix products, arithmetic and copies ran while one was open for 11% of the time, Pallas kernels for 0%

profile of v1, /device:TPU:1, one launch (start us, length us, event | category | flops | bytes accessed | tf_op | source)
XLA Modules:
  0.0 680.0 jit_solution(14640190239749805096)
XLA Ops:
  7.3 0.7 all-gather.2.cloned.1.call-update
  8.0 0.2 copy-done.11
  8.2 0.3 fusion.167
  8.5 0.6 copy-done.13
  9.1 0.5 fusion.81
  9.6 1.6 convolution_convert_fusion.2
  11.2 2.8 convolution_convert_fusion.3
  14.0 320.6 %all-gather.2.cloned.1.call-done = bf16[8,512,4096]{2,1,0:T(8,128)(2,1)} async-done(((bf16[1,512,4096]{2,1,0:T(8,128)(2,1)}), bf16[8,512,4096]{2,1,0:T(8,128)(2,1)}) %all-gather.2.cloned.1.call-update) | async-done | bytes 33554448 | tf_op jit(solution)/shard_map/all_gather | solution.py:80
  334.6 4.7 fusion.102
  339.3 4.6 fusion.101
  344.0 4.6 fusion.100
  348.6 4.6 fusion.99
  353.2 4.7 fusion.98
  357.9 4.6 fusion.97
  362.6 4.6 fusion.96
  367.2 4.6 fusion.95
  371.8 17.6 %convert_add_fusion.3 = f32[2,128,4096]{2,1,0:T(8,128)} fusion(bf16[4096,4096]{1,0:T(8,128)(2,1)} %fusion.95, bf16[2,1,128,4096]{3,2,1,0:T(8,128)(2,1)S(1)} %copy-done.5, f32[4096]{0:T(1024)S(1)} %bitcast.161, f32[2,128]{1,0:T(2,128)S(1)} %add_rsqrt_fusion.3), kind=kOutput, calls=%fused_computation.29 | convolution fusion | flops 8596226048 | bytes 39863296 | tf_op jit(solution)/shard_map/dot_general | solution.py:33
  389.4 5.0 fusion.61
  394.4 1.5 collective-permute-start
  395.9 4.9 collective-permute-done
  400.7 3.9 fusion.84
  404.6 5.1 fusion.155
  409.8 17.4 %fusion.58 = bf16[2,128,4096]{2,1,0:T(8,128)(2,1)} fusion(f32[2,128,4096]{2,1,0:T(8,128)} %fusion.155, bf16[4096,4096]{1,0:T(8,128)(2,1)} %fusion.95, bf16[2,128,4096]{2,1,0:T(8,128)(2,1)S(1)} %copy-done.6, f32[2,128]{1,0:T(2,128)S(1)} %add_rsqrt_fusion.2, f32[4096]{0:T(1024)S(1)} %bitcast.164), kind=kOutput, calls=%fused_computation.46 | convolution fusion | flops 8598323200 | bytes 41960448 | tf_op jit(solution)/shard_map/dot_general | solution.py:33
  427.1 2.6 collective-permute-start.1
  429.8 0.2 dynamic-slice_reduce_fusion
  430.0 21.7 %collective-permute-done.1 = bf16[2,128,4096]{2,1,0:T(8,128)(2,1)} collective-permute-done((bf16[2,128,4096]{2,1,0:T(8,128)(2,1)}, bf16[2,128,4096]{2,1,0:T(8,128)(2,1)}, u32[]{:S(2)}, u32[]{:S(2)}) %collective-permute-start.1) | collective-permute-done | bytes 2097184 | tf_op jit(solution)/shard_map/ppermute | solution.py:102
  451.7 2.3 fusion.87
  454.0 5.1 fusion.152
  459.1 17.3 %fusion.55 = bf16[2,128,4096]{2,1,0:T(8,128)(2,1)} fusion(f32[2,128,4096]{2,1,0:T(8,128)} %fusion.152, bf16[4096,4096]{1,0:T(8,128)(2,1)} %fusion.95, bf16[2,128,4096]{2,1,0:T(8,128)(2,1)S(1)} %copy-done.7, f32[2,128]{1,0:T(2,128)S(1)} %add_rsqrt_fusion.1, f32[4096]{0:T(1024)S(1)} %bitcast.166), kind=kOutput, calls=%fused_computation.45 | convolution fusion | flops 8598323200 | bytes 41960448 | tf_op jit(solution)/shard_map/dot_general | solution.py:33
  476.5 2.5 collective-permute-start.2
  479.0 17.5 %fusion.6 = f32[2,128,4096]{2,1,0:T(8,128)} fusion(bf16[4096,4096]{1,0:T(8,128)(2,1)} %fusion.95, bf16[2,1,128,4096]{3,2,1,0:T(8,128)(2,1)} %param.17, bf16[2,128]{1,0:T(2,128)(2,1)S(1)} %compare_convert_fusion), kind=kOutput, calls=%fused_computation.6 | convolution fusion | flops 8590983168 | bytes 39846400 | tf_op jit(solution)/shard_map/dot_general | solution.py:33
  496.5 5.6 fusion.16
  502.1 4.2 fusion.91
  506.3 0.5 copy-done.9
  506.8 2.1 fusion.74
  508.9 1.0 collective-permute-start.3
  509.9 1.6 broadcast_select_fusion.2
  511.5 4.9 fusion.159
  516.4 18.9 %fusion.92 = (f32[2,128]{1,0:T(2,128)S(1)}, f32[2,128,4096]{2,1,0:T(8,128)}) fusion(bf16[2,128,4096]{2,1,0:T(8,128)(2,1)S(1)} %get-tuple-element.14, f32[2,128,4096]{2,1,0:T(8,128)} %fusion.159, bf16[2,128,4096]{2,1,0:T(8,128)(2,1)} %broadcast_select_fusion.2, bf16[4096,4096]{1,0:T(8,128)(2,1)} %fusion.95, f32[4096]{0:T(1024)S(1)} %bitcast.168), kind=kOutput, calls=%fused_computation.80 | convolution fusion | flops 8595177472 | bytes 46154752 | tf_op jit(solution)/shard_map/dot_general | solution.py:33
  535.3 5.8 fusion.76
  541.2 1.5 collective-permute-start.4
  542.7 0.7 fusion.138
  543.4 32.8 %collective-permute-done.4 = bf16[2,128,4096]{2,1,0:T(8,128)(2,1)} collective-permute-done((bf16[2,128,4096]{2,1,0:T(8,128)(2,1)}, bf16[2,128,4096]{2,1,0:T(8,128)(2,1)}, u32[]{:S(2)}, u32[]{:S(2)}) %collective-permute-start.4) | collective-permute-done | bytes 2097184 | tf_op jit(solution)/shard_map/ppermute | solution.py:109
  576.2 3.1 broadcast_select_fusion.1
  579.3 4.9 fusion.160
  584.3 18.9 %fusion.93 = (f32[2,128]{1,0:T(2,128)S(1)}, f32[2,128,4096]{2,1,0:T(8,128)}) fusion(bf16[2,128,4096]{2,1,0:T(8,128)(2,1)S(1)} %get-tuple-element.14, f32[2,128,4096]{2,1,0:T(8,128)} %fusion.160, bf16[2,128,4096]{2,1,0:T(8,128)(2,1)} %broadcast_select_fusion.1, bf16[4096,4096]{1,0:T(8,128)(2,1)} %fusion.95, f32[4096]{0:T(1024)S(1)} %bitcast.170), kind=kOutput, calls=%fused_computation.81 | convolution fusion | flops 8595177472 | bytes 46154752 | tf_op jit(solution)/shard_map/dot_general | solution.py:33
  603.2 5.8 fusion.78
  609.0 2.9 collective-permute-start.5
  611.9 2.7 fusion.186
  614.6 17.4 %fusion.64 = bf16[1,2,1,128,4096]{4,3,2,1,0:T(8,128)(2,1)} fusion(f32[2,128,4096]{2,1,0:T(8,128)} %fusion.186, bf16[4096,4096]{1,0:T(8,128)(2,1)} %fusion.95, bf16[2,128,4096]{2,1,0:T(8,128)(2,1)S(1)} %get-tuple-element.14, f32[2,128]{1,0:T(2,128)S(1)} %get-tuple-element.27, f32[4096]{0:T(1024)S(1)} %bitcast.171), kind=kOutput, calls=%fused_computation.50 | convolution fusion | flops 8598323200 | bytes 41960448 | tf_op jit(solution)/shard_map/dot_general | solution.py:33
  631.9 1.8 broadcast_select_fusion
  633.8 0.6 convolution_convert_fusion.4
  634.4 0.4 convolution_convert_fusion
  634.8 0.7 convolution_convert_fusion.1
  635.5 2.7 fusion.180
  638.1 0.1 copy.42
  638.3 0.1 copy.43
  638.4 1.0 pad_maximum_fusion
  639.5 4.6 all-to-all-start
  644.1 18.9 %fusion.94 = (f32[2,128]{1,0:T(2,128)S(1)}, f32[2,128,4096]{2,1,0:T(8,128)}) fusion(bf16[2,128,4096]{2,1,0:T(8,128)(2,1)S(1)} %get-tuple-element.14, f32[2,128,4096]{2,1,0:T(8,128)} %fusion.180, bf16[2,128,4096]{2,1,0:T(8,128)(2,1)} %copy-done.4, bf16[4096,4096]{1,0:T(8,128)(2,1)} %fusion.95, f32[4096]{0:T(1024)S(1)} %bitcast.173), kind=kOutput, calls=%fused_computation.82 | convolution fusion | flops 8595177472 | bytes 46154752 | tf_op jit(solution)/shard_map/dot_general | solution.py:33
  663.0 5.9 fusion.116
  669.0 1.9 convert_reduce_fusion
  670.9 0.9 copy.47
  671.8 0.9 copy.48
  (46 shorter events, 0.3 us)
Async XLA Ops:
  7.2 2.4 copy-start
  7.2 1.0 copy-start.11
  7.2 1.0 copy-start.15
  7.2 1.9 copy-start.5
  7.2 327.4 %all-gather.2.cloned.1.call-start = ((), (), s32[]{:S(2)}) async-start(), calls=%async_computation.1 | async-start | bytes 37748736 | tf_op jit(solution)/shard_map/all_gather | solution.py:80
  8.5 0.6 copy-start.13
  367.2 4.6 copy-start.10
  394.4 6.4 collective-permute-start
  404.6 5.2 copy-start.6
  409.8 20.0 %copy-start.12 = (s32[2,8]{1,0:T(2,128)S(1)}, s32[2,8]{1,0:T(2,128)}, u32[]{:S(2)}) copy-start(s32[2,8]{1,0:T(2,128)} %param.16) | copy-start | bytes 196
  427.1 24.6 %collective-permute-start.1 = (bf16[2,128,4096]{2,1,0:T(8,128)(2,1)}, bf16[2,128,4096]{2,1,0:T(8,128)(2,1)}, u32[]{:S(2)}, u32[]{:S(2)}) collective-permute-start(bf16[2,128,4096]{2,1,0:T(8,128)(2,1)} %fusion.58), channel_id=1, source_target_pairs={{8,16},{9,17},{10,18},{11,19},{12,20},{13,21},{14,22},{15,23}} | collective-permute-start | bytes 6291464 | tf_op jit(solution)/shard_map/ppermute | solution.py:102
  454.0 5.2 copy-start.7
  476.5 20.0 %copy-start.8 = (bf16[2,1,128,4096]{3,2,1,0:T(8,128)(2,1)S(1)}, bf16[2,1,128,4096]{3,2,1,0:T(8,128)(2,1)}, u32[]{:S(2)}) copy-start(bf16[2,1,128,4096]{3,2,1,0:T(8,128)(2,1)} %param.17) | copy-start | bytes 6291460
  476.5 25.6 %collective-permute-start.2 = (bf16[2,128,4096]{2,1,0:T(8,128)(2,1)}, bf16[2,128,4096]{2,1,0:T(8,128)(2,1)}, u32[]{:S(2)}, u32[]{:S(2)}) collective-permute-start(bf16[2,128,4096]{2,1,0:T(8,128)(2,1)} %fusion.55), channel_id=1, source_target_pairs={{16,24},{17,25},{18,26},{19,27},{20,28},{21,29},{22,30},{23,31}} | collective-permute-start | bytes 6291464 | tf_op jit(solution)/shard_map/ppermute | solution.py:102
  502.1 4.3 copy-start.2
  502.1 4.7 copy-start.9
  508.9 1.0 collective-permute-start.3
  541.2 35.1 %collective-permute-start.4 = (bf16[2,128,4096]{2,1,0:T(8,128)(2,1)}, bf16[2,128,4096]{2,1,0:T(8,128)(2,1)}, u32[]{:S(2)}, u32[]{:S(2)}) collective-permute-start(bf16[2,128,4096]{2,1,0:T(8,128)(2,1)} %fusion.76), channel_id=1, source_target_pairs={{16,8},{17,9},{18,10},{19,11},{20,12},{21,13},{22,14},{23,15}} | collective-permute-start | bytes 6291464 | tf_op jit(solution)/shard_map/ppermute | solution.py:109
  542.7 33.6 %copy-start.3 = (bf16[2,128,4096]{2,1,0:T(8,128)(2,1)S(1)}, bf16[2,128,4096]{2,1,0:T(8,128)(2,1)}, u32[]{:S(2)}) copy-start(bf16[2,128,4096]{2,1,0:T(8,128)(2,1)} %broadcast_select_fusion.2) | copy-start | bytes 6291460
  609.0 22.9 %collective-permute-start.5 = (bf16[2,128,4096]{2,1,0:T(8,128)(2,1)}, bf16[2,128,4096]{2,1,0:T(8,128)(2,1)}, u32[]{:S(2)}, u32[]{:S(2)}) collective-permute-start(bf16[2,128,4096]{2,1,0:T(8,128)(2,1)} %fusion.78), channel_id=1, source_target_pairs={{8,0},{9,1},{10,2},{11,3},{12,4},{13,5},{14,6},{15,7}} | collective-permute-start | bytes 6291464 | tf_op jit(solution)/shard_map/ppermute | solution.py:109
  633.7 1.7 copy-start.4
  639.5 29.5 %all-to-all-start = ((bf16[1,2,2,8,8,512]{5,2,3,1,0,4:T(2,128)(2,1)}), bf16[1,2,2,8,8,512]{5,2,3,1,0,4:T(2,128)(2,1)S(1)}, u32[]{:S(2)}, u32[]{:S(2)}) async-start(bf16[1,2,2,8,8,512]{5,2,3,1,0,4:T(2,128)(2,1)} %pad_maximum_fusion), calls=%async_computation | async-start | bytes 524288 | tf_op jit(solution)/shard_map/all_to_all | solution.py:113
  663.0 5.9 copy-start.14
  663.0 9.6 %copy-start.1 = (bf16[1,16,8,4096]{3,2,1,0:T(8,128)(2,1)S(1)}, bf16[1,16,8,4096]{3,2,1,0:T(8,128)(2,1)}, u32[]{:S(2)}) copy-start(bf16[1,16,8,4096]{3,2,1,0:T(8,128)(2,1)} %param.13) | copy-start | bytes 3145732
Sparse Core Ops, SparseCore 0:
  9.6 324.9 all-gather.1
